TPU v7x, 32 devices: a whole 2x2x4 slice. The times are simulated.
32 devices in a mesh: gx: 16 (over z, y, core), gy: 2 (over x).
Axes of the slice: x: 2, y: 2, z: 4, core: 2. Of those that a mesh axis runs over, the one named last changes fastest.
Arguments:
- populations: float32 [19, 64, 16, 128], P(None, 'gx', 'gy'), may hold values from 0.02 to 0.1
- fluid: int32 [64, 16, 128], P('gx', 'gy'), may hold values 0 or 1
Outputs:
- advanced: float32 [19, 64, 16, 128], P(None, 'gx', 'gy')
Inputs may be any that keep to these rules, and one draw needn't show every extreme that they name: 1 marks a fluid cell, 0 a solid one.
All inputs are finite; a program needn't handle non-finite values. No bound on the sum of `fluid` on one device may be relied on, other than what follows from the above.
Results may differ from a plain program's by a relative error of at most 0.0001.
Values sent between devices are 32-bit elements; how exact they have to be, the bound alone decides.
A program may use at most 64 MiB of HBM per device.

v0:
```python
import jax
import jax.numpy as jnp
import numpy as np
from jax import lax
from jax.sharding import PartitionSpec as P

STEPS = 4


VELOCITIES = np.array(
    [
        [0, 0, 0],
        [1, 0, 0],
        [-1, 0, 0],
        [0, 1, 0],
        [0, -1, 0],
        [0, 0, 1],
        [0, 0, -1],
        [1, 1, 0],
        [-1, -1, 0],
        [1, -1, 0],
        [-1, 1, 0],
        [1, 0, 1],
        [-1, 0, -1],
        [1, 0, -1],
        [-1, 0, 1],
        [0, 1, 1],
        [0, -1, -1],
        [0, 1, -1],
        [0, -1, 1],
    ]
)
OPPOSITE = [0, 2, 1, 4, 3, 6, 5, 8, 7, 10, 9, 12, 11, 14, 13, 16, 15, 18, 17]
WEIGHTS = [1.0 / 3.0] + [1.0 / 18.0] * 6 + [1.0 / 36.0] * 12
relax_rate = 1.25


def padded(cells, sides, width, closed):
    for axis, dim in sides:
        count = lax.axis_size(axis)
        ends = count if closed else count - 1
        head = lax.slice_in_dim(cells, 0, width, axis=dim)
        tail = lax.slice_in_dim(cells, cells.shape[dim] - width, cells.shape[dim], axis=dim)
        cells = jnp.concatenate(
            [
                lax.ppermute(tail, axis, [(i, (i + 1) % count) for i in range(ends)]),
                cells,
                lax.ppermute(head, axis, [((i + 1) % count, i) for i in range(ends)]),
            ],
            axis=dim,
        )
    return cells


def collide(pops, wet):
    vel = jnp.asarray(VELOCITIES.T.astype(np.float32))
    weights = jnp.asarray(np.array(WEIGHTS, np.float32))
    rho = jnp.sum(pops, axis=0)
    moment = jnp.einsum("dq,qabz->dabz", vel, pops, precision=lax.Precision.HIGHEST)
    speed = moment / rho[None]
    usq = jnp.sum(speed * speed, axis=0)
    proj = jnp.einsum("dq,dabz->qabz", vel, speed, precision=lax.Precision.HIGHEST)
    feq = (
        weights[:, None, None, None]
        * rho[None]
        * (1.0 + 3.0 * proj + 4.5 * proj * proj - 1.5 * usq[None])
    )
    return jnp.where(wet[None], pops + relax_rate * (feq - pops), pops)


def stream(post, wet):
    sizea, sizeb = (post.shape[1], post.shape[2])
    here = wet[1:-1, 1:-1]
    result = []
    for q in range(19):
        cx, cy, cz = (int(VELOCITIES[q, 0]), int(VELOCITIES[q, 1]), int(VELOCITIES[q, 2]))
        source = jnp.roll(post[q, 1 - cx : sizea - 1 - cx, 1 - cy : sizeb - 1 - cy], cz, axis=-1)
        source_wet = jnp.roll(wet[1 - cx : sizea - 1 - cx, 1 - cy : sizeb - 1 - cy], cz, axis=-1)
        bounced = post[OPPOSITE[q], 1:-1, 1:-1]
        result.append(jnp.where(here, jnp.where(source_wet, source, bounced), post[q, 1:-1, 1:-1]))
    return jnp.stack(result)


def lattice_step(pops, wet):
    return stream(collide(pops, wet), wet)


def per_device(populations, fluid):
    marks = fluid.astype(jnp.float32)[None]
    stacked = jnp.concatenate([populations, marks], axis=0)
    streamwise = padded(stacked, (("gx", 1),), STEPS, True)
    extended = padded(streamwise, (("gy", 2),), STEPS, False)
    current = extended[:19]
    wet = extended[19] > 0.5
    for step in range(STEPS):
        current = lattice_step(current, wet)
        wet = wet[1:-1, 1:-1]
    return current


def solution(mesh):
    return jax.shard_map(
        per_device,
        mesh=mesh,
        in_specs=(P(None, "gx", "gy", None), P("gx", "gy", None)),
        out_specs=P(None, "gx", "gy", None),
        check_vma=False,
    )
```

profile of v0, /device:TPU:1, one launch (start us, length us, event | category | flops | bytes accessed | tf_op | source)
XLA Modules:
  0.0 62.2 jit_solution(13517468563973197698)
XLA Ops:
  0.0 0.7 %convert_bitcast_fusion = f32[1,4,8,128]{3,2,1,0:T(8,128)S(1)} fusion(s32[4,8,128]{2,1,0:T(8,128)} %param.11), kind=kLoop, calls=%fused_computation.511 | loop fusion | flops 4096 | bytes 32768 | tf_op jit(solution)/shard_map/broadcast_in_dim | solution.py:89
  0.7 1.0 %pad_maximum_fusion.6 = f32[20,4,8,128]{3,2,1,0:T(8,128)S(1)} fusion(f32[1,4,8,128]{3,2,1,0:T(8,128)S(1)} %convert_bitcast_fusion, f32[19,4,8,128]{3,2,1,0:T(8,128)} %param.10), kind=kLoop, calls=%fused_computation.52 | loop fusion | flops 81920 | bytes 655360 | tf_op jit(solution)/shard_map/concatenate | solution.py:90
  1.7 2.7 %collective-permute-start = (f32[20,4,8,128]{3,2,1,0:T(8,128)S(1)}, f32[20,4,8,128]{3,2,1,0:T(8,128)S(1)}, u32[]{:S(2)}, u32[]{:S(2)}) collective-permute-start(f32[20,4,8,128]{3,2,1,0:T(8,128)S(1)} %pad_maximum_fusion.6), channel_id=1, source_target_pairs={{0,2},{2,4},{4,6},{6,8},{8,10},{10,12},{12,14},{14,16},{16,18},{18... | collective-permute-start | bytes 983048 | tf_op jit(solution)/shard_map/ppermute | solution.py:46
  4.4 7.5 %collective-permute-done = f32[20,4,8,128]{3,2,1,0:T(8,128)S(1)} collective-permute-done((f32[20,4,8,128]{3,2,1,0:T(8,128)S(1)}, f32[20,4,8,128]{3,2,1,0:T(8,128)S(1)}, u32[]{:S(2)}, u32[]{:S(2)}) %collective-permute-start) | collective-permute-done | bytes 327712 | tf_op jit(solution)/shard_map/ppermute | solution.py:46
  11.9 2.5 %collective-permute-done.1 = f32[20,4,8,128]{3,2,1,0:T(8,128)S(1)} collective-permute-done((f32[20,4,8,128]{3,2,1,0:T(8,128)S(1)}, f32[20,4,8,128]{3,2,1,0:T(8,128)S(1)}, u32[]{:S(2)}, u32[]{:S(2)}) %collective-permute-start.1) | collective-permute-done | bytes 327712 | tf_op jit(solution)/shard_map/ppermute | solution.py:48
  14.4 1.0 %pad_maximum_fusion.5 = f32[20,12,8,128]{3,2,1,0:T(8,128)S(1)} fusion(f32[20,4,8,128]{3,2,1,0:T(8,128)S(1)} %collective-permute-done.1, f32[1,4,8,128]{3,2,1,0:T(8,128)S(1)} %convert_bitcast_fusion, f32[19,4,8,128]{3,2,1,0:T(8,128)} %param.10, f32[20,4,8,128]{3,2,1,0:T(8,128)S(1)} %collective-permute-done), kind=kLoop, calls=%fused_computation.42 | loop fusion | flops 737280 | bytes 1966080 | tf_op jit(solution)/shard_map/concatenate | solution.py:44
  15.4 0.2 fusion.298
  15.6 3.1 %collective-permute-start.2 = (f32[20,12,4,128]{3,2,1,0:T(4,128)S(1)}, f32[20,12,4,128]{3,2,1,0:T(4,128)S(1)}, u32[]{:S(2)}, u32[]{:S(2)}) collective-permute-start(f32[20,12,4,128]{3,2,1,0:T(4,128)S(1)} %get-tuple-element.121), channel_id=1, source_target_pairs={{0,1},{2,3},{4,5},{6,7},{8,9},{10,11},{12,13},{14,15},{16,17},{18,... | collective-permute-start | bytes 1474568 | tf_op jit(solution)/shard_map/ppermute | solution.py:46
  18.8 1.3 %collective-permute-start.3 = (f32[20,12,4,128]{3,2,1,0:T(4,128)S(1)}, f32[20,12,4,128]{3,2,1,0:T(4,128)S(1)}, u32[]{:S(2)}, u32[]{:S(2)}) collective-permute-start(f32[20,12,4,128]{3,2,1,0:T(4,128)S(1)} %get-tuple-element.122), channel_id=1, source_target_pairs={{1,0},{3,2},{5,4},{7,6},{9,8},{11,10},{13,12},{15,14},{17,16},{19,... | collective-permute-start | bytes 1474568 | tf_op jit(solution)/shard_map/ppermute | solution.py:48
  20.1 8.3 %collective-permute-done.2 = f32[20,12,4,128]{3,2,1,0:T(4,128)S(1)} collective-permute-done((f32[20,12,4,128]{3,2,1,0:T(4,128)S(1)}, f32[20,12,4,128]{3,2,1,0:T(4,128)S(1)}, u32[]{:S(2)}, u32[]{:S(2)}) %collective-permute-start.2) | collective-permute-done | bytes 491552 | tf_op jit(solution)/shard_map/ppermute | solution.py:46
  28.4 4.1 %collective-permute-done.3 = f32[20,12,4,128]{3,2,1,0:T(4,128)S(1)} collective-permute-done((f32[20,12,4,128]{3,2,1,0:T(4,128)S(1)}, f32[20,12,4,128]{3,2,1,0:T(4,128)S(1)}, u32[]{:S(2)}, u32[]{:S(2)}) %collective-permute-start.3) | collective-permute-done | bytes 491552 | tf_op jit(solution)/shard_map/ppermute | solution.py:48
  32.5 0.4 fusion.295
  32.9 2.9 %multiply_reduce_fusion = (f32[12,16,128]{2,1,0:T(8,128)S(1)}, f32[3,12,16,128]{3,0,2,1:T(4,128)S(1)}) fusion(f32[12,16,128]{2,1,0:T(8,128)S(1)} %get-tuple-element.62, f32[3,19,1,1]{1,0,3,2:T(4,128)S(1)} %copy-done.1, f32[19,12,16,128]{3,2,1,0:T(8,128)S(1)} %get-tuple-element.63), kind=kOutput, calls=%fused_computation.51 | convolution fusion | flops 17006592 | bytes 2359524 | tf_op jit(solution)/shard_map/dq,qabz->dabz/dot_general | solution.py:59
  35.9 0.6 copy-done.2
  36.5 4.0 %add_select_fusion = f32[19,12,16,128]{3,0,2,1:T(8,128)S(1)} fusion(f32[19,12,16,128]{3,2,1,0:T(8,128)S(1)} %get-tuple-element.63, f32[12,16,128]{2,1,0:T(8,128)S(1)} %broadcast_multiply_fusion, f32[12,16,128]{2,1,0:T(8,128)S(1)} %get-tuple-element.62, f32[19]{0:T(128)S(1)} %copy-done.2, pred[12,16,128]{2,1,0:T(8,128)(4,1)S(1)} %fusion.46, ...), kind=kOutput, calls=%fused_computation | convolution fusion | flops 22413312 | bytes 4251952 | tf_op jit(solution)/shard_map/dq,dabz->qabz/dot_general | solution.py:62
  40.5 0.8 %fusion.297 = (f32[1,10,14,128]{3,0,2,1:T(1,128)S(1)}, f32[1,10,14,128]{3,0,2,1:T(1,128)S(1)}, f32[1,10,14,128]{3,0,2,1:T(1,128)S(1)}, f32[1,10,14,128]{3,0,2,1:...) fusion(f32[19,12,16,128]{3,0,2,1:T(8,128)S(1)} %add_select_fusion), kind=kLoop, calls=%fused_computation.514 | loop fusion | bytes 2293760 | tf_op jit(solution)/shard_map/slice | solution.py:77
  41.3 0.9 %fusion.296 = (f32[1,10,14,128]{3,0,2,1:T(1,128)S(1)}, f32[1,10,14,128]{3,0,2,1:T(1,128)S(1)}, f32[1,10,14,128]{3,0,2,1:T(1,128)S(1)}, f32[1,10,14,128]{3,0,2,1:...) fusion(f32[19,12,16,128]{3,0,2,1:T(8,128)S(1)} %add_select_fusion), kind=kLoop, calls=%fused_computation.513 | loop fusion | bytes 2723840 | tf_op jit(solution)/shard_map/slice | solution.py:77
  42.2 0.2 fusion.305
  42.4 0.2 fusion.306
  42.6 0.2 fusion.303
  42.8 0.2 fusion.304
  43.0 0.1 fusion.301
  43.1 0.1 fusion.302
  43.3 0.1 fusion.299
  43.4 0.1 fusion.300
  43.6 0.1 slice.1660
  43.8 0.1 slice.1689
  44.0 0.1 slice.1701
  44.2 0.1 slice.1713
  44.5 0.9 %fusion.108 = (f32[10,14,128]{2,1,0:T(8,128)S(1)}, f32[1,10,14,128]{3,2,1,0:T(8,128)S(1)}, f32[1,10,14,128]{3,2,1,0:T(8,128)S(1)}, f32[1,10,14,128]{3,2,1,0:T(8,...) fusion(f32[1,10,14,128]{3,0,2,1:T(1,128)S(1)} %get-tuple-elemen, ...), kind=kLoop, calls=%fused_computation.240 | loop fusion | flops 1326080 | bytes 4354560 | tf_op jit(solution)/shard_map/mul | solution.py:64
  45.7 2.3 %multiply_reduce_fusion.1 = (f32[10,14,128]{2,1,0:T(8,128)S(1)}, f32[3,10,14,128]{3,0,2,1:T(4,128)S(1)}) fusion(f32[10,14,128]{2,1,0:T(8,128)S(1)} %get-tuple-element.43, f32[3,19,1,1]{1,0,3,2:T(4,128)S(1)} %copy-done.1, f32[19,10,14,128]{3,2,1,0:T(8,128)S(1)} %constant_dynamic-update-slice_fusion), kind=kOutput, calls=%fused_computation.53 | convolution fusion | flops 12400640 | bytes 1720548 | tf_op jit(solution)/shard_map/dq,qabz->dabz/dot_general | solution.py:59
  48.0 1.6 %fusion.307 = f32[19,10,14,128]{3,0,2,1:T(8,128)S(1)} fusion(f32[3,19,1,1]{1,0,3,2:T(4,128)S(1)} %copy-done.1, f32[3,10,14,128]{3,0,2,1:T(4,128)S(1)} %get-tuple-element.218), kind=kOutput, calls=%fused_computation.524 | convolution fusion | flops 12257280 | bytes 1577188 | tf_op jit(solution)/shard_map/dq,dabz->qabz/dot_general | solution.py:62
  49.6 0.7 %add_select_fusion.1 = f32[19,10,14,128]{3,2,1,0:T(8,128)S(1)} fusion(f32[19,10,14,128]{3,2,1,0:T(8,128)S(1)} %constant_dynamic-update-slice_fusion, f32[19,10,14,128]{3,0,2,1:T(8,128)S(1)} %fusion.307, f32[10,14,128]{2,1,0:T(8,128)S(1)} %broadcast_multiply_fusion.1, f32[10,14,128]{2,1,0:T(8,128)S(1)} %get-tuple-element.43, f32[19]{0:T(128)S(1)} %copy-done.2, ...), kind=kLoop, calls=%fused_computation.9 | loop fusion | flops 4085760 | bytes 4247116 | tf_op jit(solution)/shard_map/jit(_where)/select_n | solution.py:68
  50.4 0.1 slice.1743
  50.5 0.1 slice.1760
  50.6 0.1 slice.1767
  50.7 0.1 slice.1772
  50.8 0.1 slice.1779
  50.9 0.1 slice.1784
  50.9 0.1 slice.1791
  51.0 0.1 slice.1796
  51.1 0.1 slice.1803
  51.2 0.7 %add_bitcast_fusion = (f32[8,12,128]{2,1,0:T(8,128)S(1)}, f32[1,8,12,128]{3,2,1,0:T(8,128)S(1)}, f32[1,8,12,128]{3,2,1,0:T(8,128)S(1)}, f32[1,8,12,128]{3,2,1,0:...) fusion(f32[19,10,14,128]{3,2,1,0:T(8,128)S(1)} %add_select_fusi, ...), kind=kLoop, calls=%fused_computation.329 | loop fusion | flops 909312 | bytes 2985984 | tf_op jit(solution)/shard_map/mul | solution.py:64
  52.1 1.4 %multiply_reduce_fusion.2 = (f32[8,12,128]{2,1,0:T(8,128)S(1)}, f32[3,8,12,128]{3,0,2,1:T(4,128)S(1)}) fusion(f32[8,12,128]{2,1,0:T(8,128)S(1)} %get-tuple-element.24, f32[3,19,1,1]{1,0,3,2:T(4,128)S(1)} %copy-done.1, f32[19,8,12,128]{3,2,1,0:T(8,128)S(1)} %constant_dynamic-update-slice_fusion.19), kind=kOutput, calls=%fused_computation.54 | convolution fusion | flops 8503296 | bytes 1179876 | tf_op jit(solution)/shard_map/dq,qabz->dabz/dot_general | solution.py:59
  53.6 1.2 %fusion.308 = f32[19,8,12,128]{3,0,2,1:T(8,128)S(1)} fusion(f32[3,19,1,1]{1,0,3,2:T(4,128)S(1)} %copy-done.1, f32[3,8,12,128]{3,0,2,1:T(4,128)S(1)} %get-tuple-element.220), kind=kOutput, calls=%fused_computation.525 | convolution fusion | flops 8404992 | bytes 1081572 | tf_op jit(solution)/shard_map/dq,dabz->qabz/dot_general | solution.py:62
  54.8 0.5 add_select_fusion.2
  55.5 0.1 slice.1843
  55.6 0.1 slice.1850
  55.7 0.1 slice.1855
  55.8 0.1 slice.1862
  55.8 0.1 slice.1867
  56.2 0.5 add_bitcast_fusion.1
  56.9 0.9 %multiply_reduce_fusion.3 = (f32[6,10,128]{2,1,0:T(8,128)S(1)}, f32[3,6,10,128]{3,0,2,1:T(4,128)S(1)}) fusion(f32[6,10,128]{2,1,0:T(8,128)S(1)} %get-tuple-element.5, f32[3,19,1,1]{1,0,3,2:T(4,128)S(1)} %copy-done.1, f32[19,6,10,128]{3,2,1,0:T(8,128)S(1)} %constant_dynamic-update-slice_fusion.38), kind=kOutput, calls=%fused_computation.131 | convolution fusion | flops 5314560 | bytes 737508 | tf_op jit(solution)/shard_map/dq,qabz->dabz/dot_general | solution.py:59
  57.9 0.8 %fusion.309 = f32[19,6,10,128]{3,0,2,1:T(8,128)S(1)} fusion(f32[3,19,1,1]{1,0,3,2:T(4,128)S(1)} %copy-done.1, f32[3,6,10,128]{3,0,2,1:T(4,128)S(1)} %get-tuple-element.222), kind=kOutput, calls=%fused_computation.526 | convolution fusion | flops 5253120 | bytes 676068 | tf_op jit(solution)/shard_map/dq,dabz->qabz/dot_general | solution.py:62
  58.7 0.4 add_select_fusion.3
  59.3 0.1 slice_bitcast_fusion.68
  59.4 0.1 constant_dynamic-update-slice_fusion.69
  60.2 0.1 constant_dynamic-update-slice_fusion.64
  60.3 0.1 constant_dynamic-update-slice_fusion.63
  60.3 0.1 constant_dynamic-update-slice_fusion.62
  60.4 0.1 constant_dynamic-update-slice_fusion.61
  60.5 0.1 constant_dynamic-update-slice_fusion.60
  60.8 0.7 %copy-done.3 = f32[19,4,8,128]{3,2,1,0:T(8,128)} copy-done((f32[19,4,8,128]{3,2,1,0:T(8,128)}, f32[19,4,8,128]{3,2,1,0:T(8,128)S(1)}, u32[]{:S(2)}) %copy-start.3) | copy-done | bytes 311320
  61.5 0.7 %constant_dynamic-update-slice_fusion.57 = f32[19,4,8,128]{3,2,1,0:T(8,128)} fusion(f32[19,4,8,128]{3,2,1,0:T(8,128)} %copy-done.3, f32[4,8,127]{2,1,0:T(8,128)S(1)} %bitcast.1241, f32[4,8,1]{2,1,0:T(8,128)S(1)} %slice.1970, pred[4,8,127]{2,1,0:T(8,128)(4,1)S(1)} %get-tuple-element.145, pred[4,8,1]{2,1,0:T(8,128)(4,1)S(1)} %get-tuple-element.135, ...), kind=kLoop, calls=%fused_computation.112 | loop fusion | flops 16384 | bytes 73728 | tf_op jit(solution)/shard_map/stack | solution.py:81
  (111 shorter events, 2.7 us)
Async XLA Ops:
  1.7 30.8 %copy-start = (f32[19,4,8,128]{3,2,1,0:T(8,128)S(1)}, f32[19,4,8,128]{3,2,1,0:T(8,128)}, u32[]{:S(2)}) copy-start(f32[19,4,8,128]{3,2,1,0:T(8,128)} %param.10) | copy-start | bytes 933892
  1.7 10.2 %collective-permute-start = (f32[20,4,8,128]{3,2,1,0:T(8,128)S(1)}, f32[20,4,8,128]{3,2,1,0:T(8,128)S(1)}, u32[]{:S(2)}, u32[]{:S(2)}) collective-permute-start(f32[20,4,8,128]{3,2,1,0:T(8,128)S(1)} %pad_maximum_fusion.6), channel_id=1, source_target_pairs={{0,2},{2,4},{4,6},{6,8},{8,10},{10,12},{12,14},{14,16},{16,18},{18... | collective-permute-start | bytes 983048 | tf_op jit(solution)/shard_map/ppermute | solution.py:46
  4.4 10.0 %collective-permute-start.1 = (f32[20,4,8,128]{3,2,1,0:T(8,128)S(1)}, f32[20,4,8,128]{3,2,1,0:T(8,128)S(1)}, u32[]{:S(2)}, u32[]{:S(2)}) collective-permute-start(f32[20,4,8,128]{3,2,1,0:T(8,128)S(1)} %pad_maximum_fusion.6), channel_id=1, source_target_pairs={{2,0},{4,2},{6,4},{8,6},{10,8},{12,10},{14,12},{16,14},{18,16},{20... | collective-permute-start | bytes 983048 | tf_op jit(solution)/shard_map/ppermute | solution.py:48
  15.6 12.8 %collective-permute-start.2 = (f32[20,12,4,128]{3,2,1,0:T(4,128)S(1)}, f32[20,12,4,128]{3,2,1,0:T(4,128)S(1)}, u32[]{:S(2)}, u32[]{:S(2)}) collective-permute-start(f32[20,12,4,128]{3,2,1,0:T(4,128)S(1)} %get-tuple-element.121), channel_id=1, source_target_pairs={{0,1},{2,3},{4,5},{6,7},{8,9},{10,11},{12,13},{14,15},{16,17},{18,... | collective-permute-start | bytes 1474568 | tf_op jit(solution)/shard_map/ppermute | solution.py:46
  18.8 14.1 %copy-start.1 = (f32[3,19,1,1]{1,0,3,2:T(4,128)S(1)}, f32[3,19,1,1]{1,0,3,2:T(4,128)}, u32[]{:S(2)}) copy-start(f32[3,19,1,1]{1,0,3,2:T(4,128)} %constant.4) | copy-start | bytes 688
  18.8 13.7 %collective-permute-start.3 = (f32[20,12,4,128]{3,2,1,0:T(4,128)S(1)}, f32[20,12,4,128]{3,2,1,0:T(4,128)S(1)}, u32[]{:S(2)}, u32[]{:S(2)}) collective-permute-start(f32[20,12,4,128]{3,2,1,0:T(4,128)S(1)} %get-tuple-element.122), channel_id=1, source_target_pairs={{1,0},{3,2},{5,4},{7,6},{9,8},{11,10},{13,12},{15,14},{17,16},{19,... | collective-permute-start | bytes 1474568 | tf_op jit(solution)/shard_map/ppermute | solution.py:48
  35.9 0.7 %copy-start.2 = (f32[19]{0:T(128)S(1)}, f32[19]{0:T(128)}, u32[]{:S(2)}) copy-start(f32[19]{0:T(128)} %constant.17.clone) | copy-start | bytes 232
  60.8 0.7 %copy-start.3 = (f32[19,4,8,128]{3,2,1,0:T(8,128)}, f32[19,4,8,128]{3,2,1,0:T(8,128)S(1)}, u32[]{:S(2)}) copy-start(f32[19,4,8,128]{3,2,1,0:T(8,128)S(1)} %constant_dynamic-update-slice_fusion.58) | copy-start | bytes 933892
where the time goes:
time: 62.5 us; the launch traced here: 62.2 us
  waiting for transfers between devices  22.5 us (36%)
  matrix products  15.2 us (24%)
  other arithmetic  8.38 us (13%)
  local copies, waits for them, and re-layouts  8.14 us (13%)
  starting transfers between devices  7.11 us (11%)
  between operations  0.92 us (1%)
    ppermute x2, waiting for transfers between devices, padded(): lax.ppermute(tail, axis, [(i, (i + 1) % count) for i in range(ends)])  15.8 us
    dot_general x4, matrix products, collide(): jnp.einsum('dq,qabz->dabz', vel, pops, precision=lax.Precision.HIGHEST)  7.62 us
    dot_general x4, matrix products, collide(): jnp.einsum('dq,dabz->qabz', vel, speed, precision=lax.Precision.HIGHEST)  7.55 us
    ppermute x2, waiting for transfers between devices, padded(): lax.ppermute(head, axis, [((i + 1) % count, i) for i in range(ends)])  6.62 us
    ppermute x2, starting transfers between devices, padded(): lax.ppermute(tail, axis, [(i, (i + 1) % count) for i in range(ends)])  5.82 us
    slice x40, local copies, waits for them, and re-layouts, stream(): jnp.roll(post[q, 1 - cx:sizea - 1 - cx, 1 - cy:sizeb - 1 - cy], cz, axis=-1)  3.2 us
    mul x3, other arithmetic, collide(): weights[:, None, None, None] * rho[None]  2.04 us
    unnamed x63, local copies, waits for them, and re-layouts  1.72 us
  transfers between devices with their start and end apart: 4, of which 4 were waited for; matrix products, arithmetic and copies ran while one was open for 0% of the time, Pallas kernels for 0%

commit v1 on v0

v1 whole, which is shorter than its diff:
```python
import functools

import jax
import jax.numpy as jnp
import numpy as np
from jax import lax
from jax.experimental import pallas as pl
from jax.experimental.pallas import tpu as pltpu
from jax.sharding import PartitionSpec as P

STEPS = 4
DEPTH = 2
PAD = 8
RELAX = 1.25

VEL = [
    (0, 0, 0), (0, 0, 1), (0, 0, -1),
    (0, -1, 0), (0, -1, 1), (0, -1, -1),
    (0, 1, 0), (0, 1, 1), (0, 1, -1),
    (1, 1, 0), (1, 0, 0), (1, 0, 1), (1, 0, -1), (1, -1, 0),
    (-1, -1, 0), (-1, 0, 0), (-1, 0, 1), (-1, 0, -1), (-1, 1, 0),
]
REFERENCE_VEL = [
    (0, 0, 0), (1, 0, 0), (-1, 0, 0), (0, 1, 0), (0, -1, 0), (0, 0, 1), (0, 0, -1),
    (1, 1, 0), (-1, -1, 0), (1, -1, 0), (-1, 1, 0), (1, 0, 1), (-1, 0, -1),
    (1, 0, -1), (-1, 0, 1), (0, 1, 1), (0, -1, -1), (0, 1, -1), (0, -1, 1),
]
TO_REF = [REFERENCE_VEL.index(v) for v in VEL]
OPP = [VEL.index((-x, -y, -z)) for x, y, z in VEL]
WEIGHT = [(1.0 / 3.0, 1.0 / 18.0, 1.0 / 36.0)[abs(x) + abs(y) + abs(z)] for x, y, z in VEL]
DIRECTIONS = [(1, 0), (-1, 0), (0, 1), (0, -1), (1, 1), (1, -1), (-1, 1), (-1, -1)]


def runs(dx, dy):
    picks = [q for q in range(19) if (not dx or VEL[q][0] == dx) and (not dy or VEL[q][1] == dy)]
    result = []
    for q in picks:
        if result and result[-1][1] == q:
            result[-1][1] = q + 1
        else:
            result.append([q, q + 1])
    return result


def spans(d, offset, length, depth):
    if d == 0:
        return [(offset, offset, length, False)]
    inner = depth - 1
    if d > 0:
        full = (offset + length - inner, offset - inner, inner, False)
        edge = (offset + length - depth, offset - depth, 1, True)
    else:
        full = (offset, offset + length, inner, False)
        edge = (offset + inner, offset + length + inner, 1, True)
    return [full, edge] if inner else [edge]


def pieces(dx, dy, sizes, depth):
    lx, ly = sizes
    result = []
    for xs, xt, xn, xedge in spans(dx, depth, lx, depth):
        for ys, yt, yn, yedge in spans(dy, PAD, ly, depth):
            for lo, hi in runs(dx if xedge else 0, dy if yedge else 0):
                result.append((lo, hi - lo, xs, xt, xn, ys, yt, yn))
    return result


def mark_piece(dx, dy, sizes, depth):
    def along(d, offset, length):
        if d == 0:
            return offset, offset, length
        if d > 0:
            return offset + length - depth, offset - depth, depth
        return offset, offset + length, depth

    return along(dx, depth, sizes[0]) + along(dy, PAD, sizes[1])


def collide(f):
    pairs = [(q, OPP[q]) for q in range(1, 19) if q < OPP[q]]
    rho = f[0]
    moment = [None, None, None]
    for i, j in pairs:
        rho = rho + (f[i] + f[j])
        diff = f[i] - f[j]
        for axis in range(3):
            c = VEL[i][axis]
            if c:
                term = moment[axis]
                if term is None:
                    moment[axis] = diff if c > 0 else -diff
                else:
                    moment[axis] = term + diff if c > 0 else term - diff
    inverse = 1.0 / rho
    u = [m * inverse for m in moment]
    base = 1.0 - 1.5 * (u[0] * u[0] + u[1] * u[1] + u[2] * u[2])
    scaled = {w: (RELAX * w) * rho for w in set(WEIGHT)}
    keep = 1.0 - RELAX
    post = [None] * 19
    post[0] = keep * f[0] + scaled[WEIGHT[0]] * base
    for i, j in pairs:
        proj = None
        for axis in range(3):
            c = VEL[i][axis]
            if c:
                if proj is None:
                    proj = u[axis] if c > 0 else -u[axis]
                else:
                    proj = proj + u[axis] if c > 0 else proj - u[axis]
        even = scaled[WEIGHT[i]] * (base + 4.5 * (proj * proj))
        odd = scaled[WEIGHT[i]] * (3.0 * proj)
        post[i] = keep * f[i] + (even + odd)
        post[j] = keep * f[j] + (even - odd)
    return post


def row_starts(ring, ly):
    first, last = PAD - ring, PAD + ly + ring
    starts = list(range(first, last - 7, 8))
    if starts[-1] + 8 < last:
        starts.append(last - 8)
    return starts


def stream(buf, marks, layer, row):
    result = []
    for q, (cx, cy, cz) in enumerate(VEL):
        if q == 0:
            result.append(buf[0, layer, pl.ds(row, 8), :])
            continue
        source = buf[q, layer - cx, pl.ds(row - cy, 8), :]
        if cz:
            source = pltpu.roll(source, cz % source.shape[-1], 1)
        open_ = marks[cz % 3, layer - cx, pl.ds(row - cy, 8), :] != 0
        result.append(jnp.where(open_, source, buf[OPP[q], layer, pl.ds(row, 8), :]))
    return result


def kernel(axes, sizes, depth, pops_hbm, fluid_hbm, out_hbm, first, last_f, marks, *rest):
    rounds = STEPS // depth
    bufs, rest = rest[:rounds], rest[rounds:]
    inner, rest = rest[: depth - 1], rest[depth - 1 :]
    in_sem, out_sem, mark_send, mark_recv, send_sem, recv_sem = rest
    lx, ly = sizes
    nx, ny = axes
    ix, iy = lax.axis_index("gx"), lax.axis_index("gy")
    has = {0: None, 1: iy < ny - 1, -1: iy > 0}

    def when(condition, action):
        if condition is None:
            action()
        else:
            pl.when(condition)(action)

    def target(dx, dy):
        return {"gx": lax.rem(ix + nx + dx, nx), "gy": iy + dy}

    fluid_in = pltpu.make_async_copy(
        fluid_hbm, marks.at[0, pl.ds(depth, lx), pl.ds(PAD, ly)], in_sem.at[lx]
    )
    fluid_in.start()
    loads = [
        pltpu.make_async_copy(pops_hbm.at[:, a], first.at[:, a], in_sem.at[a]) for a in range(lx)
    ]
    for load in loads:
        load.start()

    barrier = pltpu.get_barrier_semaphore()
    for dx, dy in DIRECTIONS:
        when(
            has[dy],
            lambda dx=dx, dy=dy: pl.semaphore_signal(
                barrier, inc=1, device_id=target(dx, dy), device_id_type=pl.DeviceIdType.MESH
            ),
        )

    for edge, rows in ((iy == 0, PAD - depth), (iy == ny - 1, PAD + ly)):

        @pl.when(edge)
        def _():
            for a in range(lx + 2 * depth):
                marks[0, a, rows : rows + depth, :] = jnp.zeros((depth, marks.shape[-1]), jnp.int32)

    def post_layer(a):
        f = [first[TO_REF[q], a] for q in range(19)]
        for q, value in enumerate(collide(f)):
            bufs[0][q, depth + a, PAD : PAD + ly, :] = value

    order = sorted(range(lx), key=lambda a: min(a, lx - 1 - a))
    for a in order:
        loads[a].wait()
        post_layer(a)
    fluid_in.wait()

    peers = 2 + 3 * (iy > 0).astype(jnp.int32) + 3 * (iy < ny - 1).astype(jnp.int32)
    pl.semaphore_wait(barrier, peers)

    def exchange(copies):
        for (dx, dy), group in copies:
            when(has[dy], lambda group=group: [c.start() for c in group] and None)

    def arrive(copies):
        for (dx, dy), group in copies:
            when(has[-dy], lambda group=group: [c.wait_recv() for c in group] and None)

    def drain(copies):
        for (dx, dy), group in copies:
            when(has[dy], lambda group=group: [c.wait_send() for c in group] and None)

    def mark_copies():
        result = []
        for i, (dx, dy) in enumerate(DIRECTIONS):
            xs, xt, xn, ys, yt, yn = mark_piece(dx, dy, sizes, depth)
            result.append(
                (
                    (dx, dy),
                    [
                        pltpu.make_async_remote_copy(
                            src_ref=marks.at[0, pl.ds(xs, xn), pl.ds(ys, yn)],
                            dst_ref=marks.at[0, pl.ds(xt, xn), pl.ds(yt, yn)],
                            send_sem=mark_send.at[i],
                            recv_sem=mark_recv.at[i],
                            device_id=target(dx, dy),
                            device_id_type=pl.DeviceIdType.MESH,
                        )
                    ],
                )
            )
        return result

    def halo_copies(turn):
        buf = bufs[turn]
        result, count = [], 0
        for dx, dy in DIRECTIONS:
            group = []
            for lo, n, xs, xt, xn, ys, yt, yn in pieces(dx, dy, sizes, depth):
                group.append(
                    pltpu.make_async_remote_copy(
                        src_ref=buf.at[pl.ds(lo, n), pl.ds(xs, xn), pl.ds(ys, yn)],
                        dst_ref=buf.at[pl.ds(lo, n), pl.ds(xt, xn), pl.ds(yt, yn)],
                        send_sem=send_sem.at[turn, count],
                        recv_sem=recv_sem.at[turn, count],
                        device_id=target(dx, dy),
                        device_id_type=pl.DeviceIdType.MESH,
                    )
                )
                count += 1
            result.append(((dx, dy), group))
        return result

    mark_list = mark_copies()
    exchange(mark_list)
    halos = [halo_copies(turn) for turn in range(rounds)]
    exchange(halos[0])

    arrive(mark_list)
    for a in range(lx + 2 * depth):
        for row in row_starts(depth, ly):
            here = marks[0, a, row : row + 8, :]
            lanes = here.shape[-1]
            marks[1, a, row : row + 8, :] = pltpu.roll(here, 1, 1)
            marks[2, a, row : row + 8, :] = pltpu.roll(here, lanes - 1, 1)

    stores = []
    for turn in range(rounds):
        arrive(halos[turn])
        source = bufs[turn]
        for ring in range(depth - 1, -1, -1):
            final = turn == rounds - 1 and ring == 0
            for a in range(-ring, lx + ring):
                for row in row_starts(ring, ly):
                    f = stream(source, marks, depth + a, row)
                    if final:
                        wet = marks[0, depth + a, row : row + 8, :] != 0
                        for q in range(19):
                            old = first[TO_REF[q], a, row - PAD : row - PAD + 8, :]
                            last_f[TO_REF[q], a, row - PAD : row - PAD + 8, :] = jnp.where(
                                wet, f[q], old
                            )
                    else:
                        into = inner[ring - 1] if ring else bufs[turn + 1]
                        for q, value in enumerate(collide(f)):
                            into[q, depth + a, row : row + 8, :] = value
                if final:
                    store = pltpu.make_async_copy(last_f.at[:, a], out_hbm.at[:, a], out_sem.at[a])
                    store.start()
                    stores.append(store)
            if ring:
                source = inner[ring - 1]
        if turn + 1 < rounds:
            exchange(halos[turn + 1])
    drain(mark_list)
    for turn in range(rounds):
        drain(halos[turn])
    for store in stores:
        store.wait()


def per_device(axes, depth, populations, fluid):
    sizes = fluid.shape[:2]
    lx, ly = sizes
    nz = fluid.shape[2]
    rounds = STEPS // depth
    wide = (lx + 2 * depth, ly + 2 * PAD, nz)
    count = sum(len(pieces(dx, dy, sizes, depth)) for dx, dy in DIRECTIONS)
    dma = pltpu.SemaphoreType.DMA
    return pl.pallas_call(
        functools.partial(kernel, axes, sizes, depth),
        out_shape=jax.ShapeDtypeStruct(populations.shape, populations.dtype),
        in_specs=[pl.BlockSpec(memory_space=pl.ANY)] * 2,
        out_specs=pl.BlockSpec(memory_space=pl.ANY),
        scratch_shapes=[
            pltpu.VMEM(populations.shape, jnp.float32),
            pltpu.VMEM(populations.shape, jnp.float32),
            pltpu.VMEM((3,) + wide, jnp.int32),
        ]
        + [pltpu.VMEM((19,) + wide, jnp.float32)] * (rounds + depth - 1)
        + [
            dma((lx + 1,)),
            dma((lx,)),
            dma((len(DIRECTIONS),)),
            dma((len(DIRECTIONS),)),
            dma((rounds, count)),
            dma((rounds, count)),
        ],
        compiler_params=pltpu.CompilerParams(collective_id=0, has_side_effects=True),
    )(populations, fluid)


def solution(mesh):
    axes = (mesh.shape["gx"], mesh.shape["gy"])
    return jax.shard_map(
        functools.partial(per_device, axes, DEPTH),
        mesh=mesh,
        in_specs=(P(None, "gx", "gy", None), P("gx", "gy", None)),
        out_specs=P(None, "gx", "gy", None),
        check_vma=False,
    )
```

time: 62.5 us -> 21.9 us (0.35)
  the two profiles are of different devices: /device:TPU:1 before, /device:TPU:0 now
where the time goes in v1:
time: 21.9 us; the launch traced here: 21.7 us
  Pallas kernels  20 us (91%)
  local copies, waits for them, and re-layouts  1.71 us (8%)
    pallas_call x1, Pallas kernels, per_device(): pl.pallas_call(functools.partial(kernel, axes, sizes, depth), out_shape=j...  20 us
    unnamed x1, local copies, waits for them, and re-layouts  1.71 us

profile of v1, /device:TPU:0, one launch (start us, length us, event | category | flops | bytes accessed | tf_op | source)
XLA Modules:
  0.0 21.7 jit_solution(15705779959409052041)
XLA Ops:
  0.0 20.0 %shard_map.28 = f32[19,4,8,128]{3,2,1,0:T(8,128)} custom-call(f32[19,4,8,128]{3,2,1,0:T(8,128)} %pops_hbm.1, s32[4,8,128]{2,1,0:T(8,128)} %fluid_hbm.1), custom_call_target="tpu_custom_call" | custom-call | tf_op jit(solution)/shard_map/pallas_call | solution.py:307
  20.0 1.7 %copy.4 = f32[19,4,8,128]{3,2,1,0:T(8,128)} copy(f32[19,4,8,128]{3,2,1,0:T(8,128)} %shard_map.28) | data formatting | bytes 622592

commit v2 on v1

--- a/solution.py
+++ b/solution.py
@@ -9,7 +9,7 @@
 from jax.sharding import PartitionSpec as P
 
 STEPS = 4
-DEPTH = 2
+DEPTH = 4
 PAD = 8
 RELAX = 1.25
 
@@ -158,12 +158,9 @@
     fluid_in = pltpu.make_async_copy(
         fluid_hbm, marks.at[0, pl.ds(depth, lx), pl.ds(PAD, ly)], in_sem.at[lx]
     )
-    fluid_in.start()
     loads = [
         pltpu.make_async_copy(pops_hbm.at[:, a], first.at[:, a], in_sem.at[a]) for a in range(lx)
     ]
-    for load in loads:
-        load.start()
 
     barrier = pltpu.get_barrier_semaphore()
     for dx, dy in DIRECTIONS:
@@ -173,6 +170,10 @@
                 barrier, inc=1, device_id=target(dx, dy), device_id_type=pl.DeviceIdType.MESH
             ),
         )
+
+    fluid_in.start()
+    for load in loads:
+        load.start()
 
     for edge, rows in ((iy == 0, PAD - depth), (iy == ny - 1, PAD + ly)):
 

time: 21.9 us -> 18.5 us (0.84)
  the two profiles are of different devices: /device:TPU:0 before, /device:TPU:1 now
where the time goes in v2:
time: 18.5 us; the launch traced here: 18.3 us
  Pallas kernels  16.6 us (90%)
  local copies, waits for them, and re-layouts  1.71 us (9%)
    pallas_call x1, Pallas kernels, per_device(): pl.pallas_call(functools.partial(kernel, axes, sizes, depth), out_shape=j...  16.6 us
    unnamed x1, local copies, waits for them, and re-layouts  1.71 us

profile of v2, /device:TPU:1, one launch (start us, length us, event | category | flops | bytes accessed | tf_op | source)
XLA Modules:
  0.0 18.3 jit_solution(3463298206039673183)
XLA Ops:
  0.0 16.6 %shard_map.28 = f32[19,4,8,128]{3,2,1,0:T(8,128)} custom-call(f32[19,4,8,128]{3,2,1,0:T(8,128)} %pops_hbm.1, s32[4,8,128]{2,1,0:T(8,128)} %fluid_hbm.1), custom_call_target="tpu_custom_call" | custom-call | tf_op jit(solution)/shard_map/pallas_call | solution.py:308
  16.6 1.7 %copy.4 = f32[19,4,8,128]{3,2,1,0:T(8,128)} copy(f32[19,4,8,128]{3,2,1,0:T(8,128)} %shard_map.28) | data formatting | bytes 622592
